TPU v7x, 32 devices: a whole 2x2x4 slice. The times are simulated.
32 devices in a mesh: row: 8 (over y, x, core), col: 4 (over z).
Axes of the slice: x: 2, y: 2, z: 4, core: 2. Of those that a mesh axis runs over, the one named last changes fastest.
Arguments:
- features: bfloat16 [32768, 512], P('col', 'row'), may hold values from -6 to 6
- weight_t: bfloat16 [512, 512], P(None, 'row'), may hold values from -0.25 to 0.25
- tiles: bfloat16 [8192, 128, 128], P(('row', 'col')), may hold values from -0.15625 to 0.15625
- coords: int32 [2, 8192], P(None, ('row', 'col')), may hold values from 0 to 63, as said below
- counts: int32 [32], P(('row', 'col')), may hold values from 32 to 256, as said below
Outputs:
- output: bfloat16 [32768, 512], P('row', 'col')
Inputs may be any that keep to these rules, and one draw needn't show every extreme that they name: coords[0] of a slot lies in 0 to 31 and coords[1] in 0 to 63; the live slots of one grid cell name distinct tiles. `counts`: some grid cell has all 256 slots live in every draw.
All inputs are finite; a program needn't handle non-finite values.
Results may differ from a plain program's by a relative error of at most 0.0095.
Values may be sent and summed in bfloat16 or wider, within the bound.
No kernel may reach another device: no remote copies, remote signals or barrier semaphores. Data moves between devices by JAX's collectives and lax.ppermute only.
A program may use at most 128 MiB of HBM per device.

v0:
```python
import jax
import jax.numpy as jnp
from jax import lax
from jax.sharding import PartitionSpec as P

TROW = 32


def tile_apply(tiles, rows, cols, count, source):
    maxt = tiles.shape[0]
    tile = tiles.shape[1]
    width = source.shape[2]
    tcol_here = source.shape[0]
    group = min(32, maxt)
    offsets = jnp.arange(group, dtype=jnp.int32)
    col_lanes = jnp.arange(tcol_here, dtype=jnp.int32)
    row_lanes = jnp.arange(TROW, dtype=jnp.int32)

    def step(index, total):
        start = (index * group).astype(jnp.int32)
        block = lax.dynamic_slice_in_dim(tiles, start, group, 0)
        block_rows = lax.dynamic_slice_in_dim(rows, start, group, 0)
        block_cols = lax.dynamic_slice_in_dim(cols, start, group, 0)
        live = start + offsets < count
        pick_cols = (block_cols[:, None] == col_lanes[None, :]).astype(jnp.bfloat16)
        inputs = jnp.einsum(
            "gc,cjw->gjw", pick_cols, source, preferred_element_type=jnp.float32
        ).astype(jnp.bfloat16)
        prod = jnp.einsum("gij,gjw->giw", block, inputs, preferred_element_type=jnp.float32)
        place_rows = ((block_rows[:, None] == row_lanes[None, :]) & live[:, None]).astype(
            jnp.float32
        )
        added = jnp.einsum("gt,giw->tiw", place_rows, prod, precision=lax.Precision.HIGHEST)
        return total + added

    turns = (count + group - 1) // group
    total = lax.fori_loop(0, turns, step, jnp.zeros((TROW, tile, width), jnp.float32))
    return total.reshape(TROW * tile, width)


def body(features, weight_t, tiles, coords, counts):
    rows = coords[0]
    cols = coords[1]
    count = counts[0]
    tile = tiles.shape[1]
    tcol_here = features.shape[0] // tile
    panel, weight_full = (
        lax.all_gather(features, "row", axis=1, tiled=True),
        lax.all_gather(weight_t, "row", axis=1, tiled=True),
    )
    spread = tile_apply(tiles, rows, cols, count, panel.reshape(tcol_here, tile, panel.shape[1]))
    partial_value = lax.dot_general(
        spread,
        weight_full.astype(jnp.float32),
        (((1,), (1,)), ((), ())),
        precision=lax.Precision.HIGHEST,
    )
    summed = lax.psum_scatter(partial_value, "col", scatter_dimension=1, tiled=True)
    return summed.astype(jnp.bfloat16)


def solution(mesh):
    placed = (
        P("col", "row"),
        P(None, "row"),
        P(("row", "col"), None, None),
        P(None, ("row", "col")),
        P(("row", "col")),
    )
    return jax.shard_map(
        body, mesh=mesh, in_specs=placed, out_specs=P("row", "col"), check_vma=False
    )
```

profile of v0, /device:TPU:0, one launch (start us, length us, event | category | flops | bytes accessed | tf_op | source)
XLA Modules:
  0.0 517.2 jit_solution(8024863803451204911)
XLA Ops:
  6.5 0.0 all-gather.2.cloned.1.call-start
  6.5 0.7 all-gather.2.cloned.1.call-update
  7.3 0.0 reduce-scatter.2.cloned.1.call-start
  8.0 11.6 %all_gather.7 = bf16[512,512]{0,1:T(8,128)(2,1)S(1)} all-gather(bf16[512,64]{0,1:T(8,128)(2,1)} %param.8), channel_id=1, replica_groups=mesh['row'=8,'col'=4] {'row'}, dimensions={1}, use_global_device_ids=true | all-gather | bytes 589824 | tf_op jit(solution)/shard_map/all_gather | solution.py:49
  19.6 0.8 fusion.23
  20.4 45.9 %all-gather.2.cloned.1.call-done = bf16[8192,512]{0,1:T(8,128)(2,1)} async-done(((bf16[8192,64]{0,1:T(8,128)(2,1)}), bf16[8192,512]{0,1:T(8,128)(2,1)}) %all-gather.2.cloned.1.call-update) | async-done | bytes 8388624 | tf_op jit(solution)/shard_map/all_gather | solution.py:48
  66.2 12.0 %copy.7 = bf16[8192,512]{1,0:T(8,128)(2,1)} copy(bf16[8192,512]{0,1:T(8,128)(2,1)} %all-gather.2.cloned.1.call-done) | data formatting | bytes 16777216 | tf_op jit(solution)/shard_map/all_gather | solution.py:48
  78.2 4.3 broadcast_in_dim.13
  82.5 66.3 %while.13 = (s32[]{:T(128)}, f32[32,128,512]{2,0,1:T(8,128)}, s32[]{:T(128)}, s32[256]{0:T(256)S(1)}, s32[]{:T(128)}, /*index=5*/bf16[256,128,128]{2,1,0:T(8,128...) while((s32[]{:T(128)}, f32[32,128,512]{2,0,1:T(8,128)}, ...), condition=%wide.region_1.2_spmd.clone.clone, body=%wide.region_0.1_spmd.clone.clone.sunk | while | flops 1612713984 | bytes 51381240 | solution.py:37
  82.5 0.1 dynamic_slice.24
  82.6 13.4 %fusion.41 = bf16[32,128,512]{2,0,1:T(8,128)(2,1)S(1)} fusion(bf16[64,128,512]{2,1,0:T(8,128)(2,1)} %get-tuple-element.233, s32[32]{0:T(128)S(1)} %dynamic_slice.24), kind=kOutput, calls=%fused_computation.5.clone.1 | convolution fusion | flops 268437504 | bytes 12583040 | tf_op jit(solution)/shard_map/while/body/gc,cjw->gjw/dot_general | solution.py:26
  96.0 6.4 %fusion.42 = f32[32,128,512]{2,1,0:T(8,128)S(1)} fusion(bf16[32,128,512]{2,0,1:T(8,128)(2,1)S(1)} %fusion.41, bf16[256,128,128]{2,1,0:T(8,128)(2,1)} %get-tuple-element.231, s32[]{:T(128)S(6)} %select_n.15), kind=kOutput, calls=%fused_computation.7.clone.1 | convolution fusion | flops 536870912 | bytes 13631492 | tf_op jit(solution)/shard_map/while/body/gij,gjw->giw/dot_general | solution.py:29
  102.3 0.1 dynamic_slice.25
  102.4 0.7 fusion.43
  103.1 12.6 %fusion.44 = f32[32,128,512]{2,0,1:T(8,128)} fusion(f32[32,128,512]{2,0,1:T(8,128)} %get-tuple-element.215, f32[32,128,512]{2,1,0:T(8,128)S(1)} %fusion.42, s32[32]{0:T(128)S(1)} %dynamic_slice.25, pred[32]{0:T(512)(128)(4,1)S(1)} %fusion.43), kind=kOutput, calls=%fused_computation.8.clone.1 | convolution fusion | flops 807405568 | bytes 25165984 | tf_op jit(solution)/shard_map/while/body/gt,giw->tiw/dot_general | solution.py:33
  115.7 0.1 dynamic_slice.24
  115.7 13.4 %fusion.41 = bf16[32,128,512]{2,0,1:T(8,128)(2,1)S(1)} fusion(bf16[64,128,512]{2,1,0:T(8,128)(2,1)} %get-tuple-element.233, s32[32]{0:T(128)S(1)} %dynamic_slice.24), kind=kOutput, calls=%fused_computation.5.clone.1 | convolution fusion | flops 268437504 | bytes 12583040 | tf_op jit(solution)/shard_map/while/body/gc,cjw->gjw/dot_general | solution.py:26
  129.1 6.4 %fusion.42 = f32[32,128,512]{2,1,0:T(8,128)S(1)} fusion(bf16[32,128,512]{2,0,1:T(8,128)(2,1)S(1)} %fusion.41, bf16[256,128,128]{2,1,0:T(8,128)(2,1)} %get-tuple-element.231, s32[]{:T(128)S(6)} %select_n.15), kind=kOutput, calls=%fused_computation.7.clone.1 | convolution fusion | flops 536870912 | bytes 13631492 | tf_op jit(solution)/shard_map/while/body/gij,gjw->giw/dot_general | solution.py:29
  135.5 0.1 dynamic_slice.25
  135.5 0.7 fusion.43
  136.2 12.6 %fusion.44 = f32[32,128,512]{2,0,1:T(8,128)} fusion(f32[32,128,512]{2,0,1:T(8,128)} %get-tuple-element.215, f32[32,128,512]{2,1,0:T(8,128)S(1)} %fusion.42, s32[32]{0:T(128)S(1)} %dynamic_slice.25, pred[32]{0:T(512)(128)(4,1)S(1)} %fusion.43), kind=kOutput, calls=%fused_computation.8.clone.1 | convolution fusion | flops 807405568 | bytes 25165984 | tf_op jit(solution)/shard_map/while/body/gt,giw->tiw/dot_general | solution.py:33
  148.8 8.2 %copy.8 = f32[32,128,512]{2,1,0:T(8,128)S(1)} copy(f32[32,128,512]{2,0,1:T(8,128)} %get-tuple-element.88) | data formatting | bytes 16777216 | tf_op jit(solution)/shard_map/while | solution.py:37
  157.1 8.9 %fusion.24 = f32[4096,512]{1,0:T(8,128)} fusion(f32[4096,512]{1,0:T(8,128)S(1)} %bitcast.19, bf16[512,512]{0,1:T(8,128)(2,1)S(1)} %all_gather.7), kind=kOutput, calls=%fused_computation.22 | convolution fusion | flops 12884901888 | bytes 17301504 | tf_op jit(solution)/shard_map/dot_general | solution.py:52
  166.0 0.0 reduce-scatter.2.cloned.1.call-update
  166.0 341.7 %reduce-scatter.2.cloned.1.call-done = f32[4096,128]{1,0:T(8,128)} async-done(((f32[4096,512]{1,0:T(8,128)}), f32[4096,128]{1,0:T(8,128)}) %reduce-scatter.2.cloned.1.call-update) | async-done | bytes 2097168 | tf_op jit(solution)/shard_map/reduce_scatter | solution.py:58
  507.7 2.7 convert_element_type.12
Async XLA Ops:
  6.5 59.7 %all-gather.2.cloned.1.call-start = ((), (), s32[]{:S(2)}) async-start(), calls=%async_computation.1 | async-start | bytes 9437184 | tf_op jit(solution)/shard_map/all_gather | solution.py:48
  7.3 500.5 %reduce-scatter.2.cloned.1.call-start = ((), (), s32[]{:S(2)}) async-start(), calls=%async_computation.2 | async-start | bytes 10485760 | tf_op jit(solution)/shard_map/reduce_scatter | solution.py:58
Sparse Core Ops, SparseCore 0:
  9.2 56.9 all-gather.1
  166.1 341.5 reduce-scatter.1
where the time goes:
time: 520 us; the launch traced here: 517 us
  waiting for transfers between devices  388 us (75%)
  matrix products  73.6 us (14%)
  local copies, waits for them, and re-layouts  25.6 us (5%)
  between operations  14.1 us (3%)
  blocking collectives  11.6 us (2%)
    reduce_scatter x1, waiting for transfers between devices, body(): lax.psum_scatter(partial_value, 'col', scatter_dimension=1, tiled=True)  342 us
    all_gather x1, waiting for transfers between devices, body(): lax.all_gather(features, 'row', axis=1, tiled=True)  45.9 us
    dot_general x2, matrix products, step(): jnp.einsum('gc,cjw->gjw', pick_cols, source, preferred_element_type=jnp.f...  26.7 us
    dot_general x2, matrix products, step(): jnp.einsum('gt,giw->tiw', place_rows, prod, precision=lax.Precision.HIGHEST)  25.2 us
    dot_general x2, matrix products, step(): jnp.einsum('gij,gjw->giw', block, inputs, preferred_element_type=jnp.floa...  12.7 us
    all_gather x1, local copies, waits for them, and re-layouts, body(): lax.all_gather(features, 'row', axis=1, tiled=True)  12 us
    all_gather x1, blocking collectives, body(): lax.all_gather(weight_t, 'row', axis=1, tiled=True)  11.6 us
  transfers between devices with their start and end apart: 2, of which 2 were waited for; matrix products, arithmetic and copies ran while one was open for 0% of the time, Pallas kernels for 0%

commit v1 on v0

v1 whole, which is shorter than its diff:
```python
import functools

import jax
import jax.numpy as jnp
from jax import lax
from jax.experimental import pallas as pl
from jax.experimental.pallas import tpu as pltpu
from jax.sharding import PartitionSpec as P

SPAN = 4
GROUP = 8
FEATURE_PARTS = 2
ROW_PARTS = 2


def plan_kernel(coords, counts, slot_out, col_out, row_out, edge_out, seen, begin, *, brows, pad_col):
    count = counts[0]
    jobs = row_out.shape[0]

    def clear(r, _):
        seen[r] = 0
        return 0

    lax.fori_loop(0, brows, clear, 0)

    def tally(s, _):
        r = coords[0, s]
        seen[r] = seen[r] + 1
        return 0

    lax.fori_loop(0, count, tally, 0)

    part_rows = brows // ROW_PARTS

    def blank(j, _):
        for k in range(SPAN):
            slot_out[j * SPAN + k] = 0
            col_out[j * SPAN + k] = pad_col
        row_out[j] = 0
        return 0

    lax.fori_loop(0, jobs, blank, 0)

    edge_out[0] = 0
    at = jnp.int32(0)
    for part in range(ROW_PARTS):

        def lay(r, at):
            begin[r] = at * SPAN
            return at + (seen[r] + SPAN - 1) // SPAN

        first = at
        at = lax.fori_loop(part * part_rows, (part + 1) * part_rows, lay, at)
        at = first + (at - first + GROUP - 1) // GROUP * GROUP
        edge_out[part + 1] = at // GROUP

    def place(s, _):
        r = coords[0, s]
        spot = begin[r]
        begin[r] = spot + 1
        slot_out[spot] = s
        col_out[spot] = coords[1, s]
        row_out[spot // SPAN] = r % part_rows
        return 0

    lax.fori_loop(0, count, place, 0)


def make_plan(coords, counts, brows, bcols):
    maxt = coords.shape[1]
    jobs = brows + -(-maxt // SPAN) + ROW_PARTS * GROUP
    jobs = -(-jobs // GROUP) * GROUP
    smem = pl.BlockSpec(memory_space=pltpu.SMEM)
    ints = lambda n: jax.ShapeDtypeStruct((n,), jnp.int32)
    return pl.pallas_call(
        functools.partial(plan_kernel, brows=brows, pad_col=bcols),
        out_shape=(ints(jobs * SPAN), ints(jobs * SPAN), ints(jobs), ints(ROW_PARTS + 1)),
        in_specs=[smem, smem],
        out_specs=(smem, smem, smem, smem),
        scratch_shapes=[pltpu.SMEM((brows,), jnp.int32), pltpu.SMEM((brows,), jnp.int32)],
        name="plan",
    )(coords, counts)


def apply_tiles(slot, col, row, edge, tiles, panel, acc, tbuf, pbuf, tsem, psem, lo, hi):
    tile = tiles.shape[1]
    per = GROUP * SPAN
    nodes = panel.shape[1]
    load = pltpu.make_async_copy(panel, pbuf.at[:, pl.ds(0, nodes)], psem)
    load.start()

    def fetch(g, _):
        for k in range(per):
            s = slot[g * per + k]
            pltpu.make_async_copy(
                tiles.at[s], tbuf.at[(g - lo) * per + k], tsem.at[g - lo]
            ).start()
        return 0

    lax.fori_loop(lo, hi, fetch, 0)
    pbuf[:, pl.ds(nodes, tile)] = jnp.zeros((pbuf.shape[0], tile), pbuf.dtype)
    acc[...] = jnp.zeros_like(acc)
    load.wait()

    def work(g, _):
        own = tbuf.at[pl.ds((g - lo) * per, per)]
        pltpu.make_async_copy(tiles.at[pl.ds(0, per)], own, tsem.at[g - lo]).wait()
        for j in range(GROUP):
            job = g * GROUP + j
            base = (g - lo) * per + j * SPAN
            lhs = jnp.concatenate([tbuf[base + k] for k in range(SPAN)], axis=1)
            rhs = jnp.concatenate(
                [
                    pbuf[:, pl.ds(pl.multiple_of(col[job * SPAN + k] * tile, tile), tile)]
                    for k in range(SPAN)
                ],
                axis=1,
            )
            prod = lax.dot_general(
                lhs, rhs, (((1,), (1,)), ((), ())), preferred_element_type=jnp.float32
            )
            spot = pl.ds(pl.multiple_of(row[job] * tile, tile), tile)
            acc[spot, :] = acc[spot, :] + prod
        return 0

    lax.fori_loop(lo, hi, work, 0)


def early_kernel(slot, col, row, edge, tiles, panel, out, acc, tbuf, pbuf, tsem, psem):
    rows = acc.shape[0]
    for part in range(ROW_PARTS):
        apply_tiles(
            slot, col, row, edge, tiles, panel, acc, tbuf, pbuf, tsem, psem,
            edge[part], edge[part + 1],
        )
        out[pl.ds(part * rows, rows), :] = acc[...].astype(out.dtype)


def last_kernel(slot, col, row, edge, tiles, panel, weight, *rest, part):
    *before, out, acc, tbuf, pbuf, tsem, psem = rest
    apply_tiles(
        slot, col, row, edge, tiles, panel, acc, tbuf, pbuf, tsem, psem,
        edge[part], edge[part + 1],
    )
    rows = acc.shape[0]
    step = min(rows, 512)
    for start in range(0, rows, step):
        spot = pl.ds(start, step)
        lhs = jnp.concatenate(
            [one[spot, :] for one in before] + [acc[spot, :].astype(jnp.bfloat16)], axis=1
        )
        out[spot, :] = jnp.dot(
            lhs, weight[...], preferred_element_type=jnp.float32
        ).astype(out.dtype)


def scratch_of(rows, width, nodes, tile, jobs):
    groups = jobs // GROUP
    return [
        pltpu.VMEM((rows, width), jnp.float32),
        pltpu.VMEM((jobs * SPAN, tile, tile), jnp.bfloat16),
        pltpu.VMEM((width, nodes + tile), jnp.bfloat16),
        pltpu.SemaphoreType.DMA((groups,)),
        pltpu.SemaphoreType.DMA,
    ]


def body(features, weight_t, tiles, coords, counts):
    maxt, tile, _ = tiles.shape
    nodes, wide = features.shape
    fout = weight_t.shape[0]
    nrow, ncol = lax.axis_size("row"), lax.axis_size("col")
    out_rows = nodes * ncol // nrow
    brows, bcols = out_rows // tile, nodes // tile
    piece = wide // FEATURE_PARTS
    width = piece * nrow
    rows = out_rows // ROW_PARTS

    plan = make_plan(coords, counts, brows, bcols)
    jobs = plan[2].shape[0]
    panels = []
    for f in range(FEATURE_PARTS):
        own = features[:, f * piece : (f + 1) * piece]
        if panels:
            own, _ = lax.optimization_barrier((own, own[:1]))
        panels.append(lax.all_gather(own, "row", axis=1, tiled=True).T)
    weight = lax.all_gather(weight_t, "row", axis=1, tiled=True).T
    weight = weight.reshape(nrow, FEATURE_PARTS, piece, fout).swapaxes(0, 1)
    weight = weight.reshape(FEATURE_PARTS * width, fout)

    smem = pl.BlockSpec(memory_space=pltpu.SMEM)
    hbm = pl.BlockSpec(memory_space=pl.ANY)
    scratch = scratch_of(rows, width, nodes, tile, jobs)
    limit = pltpu.CompilerParams(vmem_limit_bytes=48 * 1024 * 1024)
    flops = 2 * maxt * tile * tile * width
    before = [
        pl.pallas_call(
            early_kernel,
            out_shape=jax.ShapeDtypeStruct((out_rows, width), jnp.bfloat16),
            in_specs=[smem] * 4 + [hbm, hbm],
            scratch_shapes=scratch,
            compiler_params=limit,
            cost_estimate=pl.CostEstimate(flops=flops, transcendentals=0, bytes_accessed=1 << 24),
            name="early",
        )(*plan, tiles, panel)
        for panel in panels[:-1]
    ]
    outs = []
    for part in range(ROW_PARTS):
        here = pl.BlockSpec((rows, width), lambda i, part=part: (part, 0))
        partial = pl.pallas_call(
            functools.partial(last_kernel, part=part),
            grid=(1,),
            out_shape=jax.ShapeDtypeStruct((rows, fout), jnp.bfloat16),
            in_specs=[smem] * 4
            + [hbm, hbm, pl.BlockSpec(weight.shape, lambda i: (0, 0))]
            + [here] * len(before),
            out_specs=pl.BlockSpec((rows, fout), lambda i: (0, 0)),
            scratch_shapes=scratch,
            compiler_params=limit,
            cost_estimate=pl.CostEstimate(flops=flops, transcendentals=0, bytes_accessed=1 << 24),
            name="last",
        )(*plan, tiles, panels[-1], weight, *before)
        outs.append(lax.psum_scatter(partial, "col", scatter_dimension=1, tiled=True))
    return jnp.concatenate(outs, axis=0).astype(jnp.bfloat16)


def solution(mesh):
    placed = (
        P("col", "row"),
        P(None, "row"),
        P(("row", "col"), None, None),
        P(None, ("row", "col")),
        P(("row", "col")),
    )
    return jax.shard_map(
        body, mesh=mesh, in_specs=placed, out_specs=P("row", "col"), check_vma=False
    )
```

time: 520 us -> 200 us (0.38)
  waiting for transfers between devices: 388 us -> 125 us
  matrix products: 73.6 us -> 0 us
  Pallas kernels: 0 us -> 29.4 us
  local copies, waits for them, and re-layouts: 25.6 us -> 18.4 us
    reduce_scatter x1 -> x0, waiting for transfers between devices: 342 us -> none  [body(): lax.psum_scatter(partial_value, 'col', scatter_dimension=1, tiled=True)]
    unnamed x2 -> x6, waiting for transfers between devices: 0.73 us -> 78.7 us
    dot_general x7 -> x0, matrix products: 73.6 us -> none  [the longest x2 26.7 us: step(): jnp.einsum('gc,cjw->gjw', pick_cols, source, preferred_element_type=jnp.f...]
    pallas_call x0 -> x4, Pallas kernels: none -> 29.4 us  [the longest x2 13.4 us: body(): pl.pallas_call(functools.partial(last_kernel, part=part), grid=(1,), out_...]
    unnamed x0 -> x26, local copies, waits for them, and re-layouts: none -> 16 us
    all_gather x1 -> x0, local copies, waits for them, and re-layouts: 12 us -> none  [body(): lax.all_gather(features, 'row', axis=1, tiled=True)]
    while x1 -> x0, local copies, waits for them, and re-layouts: 8.24 us -> none  [tile_apply(): lax.fori_loop(0, turns, step, jnp.zeros((TROW, tile, width), jnp.float32))]
    all_gather x1 -> x2, waiting for transfers between devices: 45.9 us -> 46.7 us  [body(): panels.append(lax.all_gather(own, 'row', axis=1, tiled=True).T)]
  transfers between devices with their start and end apart: 2 -> 4, of which waited for: 2 -> 4; matrix products, arithmetic and copies ran while one was open for 0% -> 3% of each run, Pallas kernels for 0% -> 12%
where the time goes in v1:
time: 200 us
  waiting for transfers between devices  125 us (62%)
  Pallas kernels  29.4 us (15%)
  local copies, waits for them, and re-layouts  18.4 us (9%)
  between operations  13.9 us (7%)
  blocking collectives  11.3 us (6%)
    unnamed x6, waiting for transfers between devices  78.7 us
    all_gather x2, waiting for transfers between devices, body(): panels.append(lax.all_gather(own, 'row', axis=1, tiled=True).T)  46.7 us
    unnamed x26, local copies, waits for them, and re-layouts  16 us
    pallas_call x2, Pallas kernels, body(): pl.pallas_call(functools.partial(last_kernel, part=part), grid=(1,), out_...  13.4 us
    all_gather x1, blocking collectives, body(): weight = lax.all_gather(weight_t, 'row', axis=1, tiled=True).T  11.3 us
    pallas_call x1, Pallas kernels, body(): pl.pallas_call(early_kernel, out_shape=jax.ShapeDtypeStruct((out_rows, wi...  10.5 us
    pallas_call x1, Pallas kernels, make_plan(): pl.pallas_call(functools.partial(plan_kernel, brows=brows, pad_col=bcols)...  5.51 us
  transfers between devices with their start and end apart: 4, of which 4 were waited for; matrix products, arithmetic and copies ran while one was open for 3% of the time, Pallas kernels for 12%

profile of v1, /device:TPU:0, one launch (start us, length us, event | category | flops | bytes accessed | tf_op | source)
XLA Modules:
  0.0 199.6 jit_solution(2348533030029795279)
XLA Ops:
  6.5 0.0 copy-start.10
  6.5 0.0 all-gather.5.cloned.1.call-start
  6.5 2.3 %fusion = (bf16[8192,32]{0,1:T(8,128)(2,1)}, bf16[8192,32]{0,1:T(8,128)(2,1)}) fusion(bf16[8192,64]{0,1:T(8,128)(2,1)} %param.5), kind=kLoop, calls=%fused_computation.1 | loop fusion | bytes 2097152 | tf_op jit(solution)/shard_map/slice | solution.py:183
  8.9 0.0 all-gather.5.cloned.1.call-update
  8.9 0.0 all-gather.3.cloned.1.call-start
  8.9 0.7 all-gather.3.cloned.1.call-update
  9.6 0.0 reduce-scatter.9.cloned.1.call-start
  10.3 0.0 copy-done.10
  10.3 11.3 %all_gather.10 = bf16[512,512]{0,1:T(8,128)(2,1)S(1)} all-gather(bf16[512,64]{0,1:T(8,128)(2,1)S(1)} %copy-done.10), channel_id=1, replica_groups=mesh['row'=8,'col'=4] {'row'}, dimensions={1}, use_global_device_ids=true | all-gather | bytes 589824 | tf_op jit(solution)/shard_map/all_gather | solution.py:187
  21.7 5.5 %plan.1 = (s32[448]{0:T(512)}, s32[448]{0:T(512)}, s32[112]{0:T(128)}, s32[3]{0:T(128)}) custom-call(s32[2,256]{1,0:T(2,128)} %coords.1, s32[1]{0:T(128)S(6)} %copy.12.counts), custom_call_target="tpu_custom_call" | custom-call | tf_op jit(solution)/shard_map/plan/pallas_call | solution.py:75
  27.2 21.3 %all-gather.5.cloned.1.call-done = bf16[8192,256]{0,1:T(8,128)(2,1)} async-done(((bf16[8192,32]{0,1:T(8,128)(2,1)}), bf16[8192,256]{0,1:T(8,128)(2,1)}) %all-gather.5.cloned.1.call-update) | async-done | bytes 4194320 | tf_op jit(solution)/shard_map/all_gather | solution.py:186
  48.6 0.0 copy-start.2
  48.6 0.6 copy-done.2
  49.2 0.0 copy-start.4
  49.2 0.7 copy-done.4
  49.9 0.0 copy-start.6
  49.9 0.7 copy-done.6
  50.5 0.0 copy-start.8
  50.5 0.6 copy-done.8
  51.2 0.0 copy-start.3
  51.2 0.0 copy-start.5
  51.2 0.0 copy-start.7
  51.2 0.0 copy-start.9
  51.2 10.5 %early.1.rest_0_ = bf16[4096,256]{1,0:T(8,128)(2,1)S(1)} custom-call(s32[448]{0:T(512)S(1)} %copy-done.2, s32[448]{0:T(512)S(1)} %copy-done.4, s32[112]{0:T(128)S(1)} %copy-done.6, s32[3]{0:T(128)S(1)} %copy-done.8, bf16[256,128,128]{2,1,0:T(8,128)(2,1)} %tiles.5, bf16[256,8192]{1,0:T(8,128)(2,1)} %bitcast.18), custom_call_target="tpu_custom_call" | custom-call | flops 2147483648 | bytes 16777216 | tf_op jit(solution)/shard_map/early/pallas_call | solution.py:197
  61.7 25.4 %all-gather.3.cloned.1.call-done = bf16[8192,256]{0,1:T(8,128)(2,1)} async-done(((bf16[8192,32]{0,1:T(8,128)(2,1)}), bf16[8192,256]{0,1:T(8,128)(2,1)}) %all-gather.3.cloned.1.call-update) | async-done | bytes 4194320 | tf_op jit(solution)/shard_map/all_gather | solution.py:186
  87.1 0.0 copy-done.3
  87.1 0.0 copy-done.5
  87.1 0.0 copy-done.7
  87.1 0.0 copy-done.9
  87.1 6.2 %last.3 = bf16[2048,512]{1,0:T(8,128)(2,1)S(1)} custom-call(s32[448]{0:T(512)S(1)} %copy-done.3, s32[448]{0:T(512)S(1)} %copy-done.5, s32[112]{0:T(128)S(1)} %copy-done.7, s32[3]{0:T(128)S(1)} %copy-done.9, bf16[256,128,128]{2,1,0:T(8,128)(2,1)} %tiles.5, bf16[256,8192]{1,0:T(8,128)(2,1)} %bitcast.14, bf16[512,512]{1,0:T(8,128)(2,1)S(1)} %bitcast.12, ...), custom_call_target="tpu_custom_call" | custom-call | flops 2147483648 | bytes 16777216 | tf_op jit(solution)/shard_map/last/pallas_call | solution.py:211
  93.3 0.0 copy-start.1
  93.3 1.3 copy-done.1
  94.7 4.0 %copy.10 = bf16[2048,512]{0,1:T(8,128)(2,1)} copy(bf16[2048,512]{1,0:T(8,128)(2,1)} %copy-done.1) | data formatting | bytes 4194304
  98.6 0.0 reduce-scatter.9.cloned.1.call-update
  98.7 0.0 reduce-scatter.7.cloned.1.call-start
  98.7 7.2 %last.2 = bf16[2048,512]{1,0:T(8,128)(2,1)S(1)} custom-call(s32[448]{0:T(512)S(1)} %copy-done.3, s32[448]{0:T(512)S(1)} %copy-done.5, s32[112]{0:T(128)S(1)} %copy-done.7, s32[3]{0:T(128)S(1)} %copy-done.9, bf16[256,128,128]{2,1,0:T(8,128)(2,1)} %tiles.5, bf16[256,8192]{1,0:T(8,128)(2,1)} %bitcast.15, bf16[512,512]{1,0:T(8,128)(2,1)S(1)} %bitcast.13, ...), custom_call_target="tpu_custom_call" | custom-call | flops 2147483648 | bytes 16777216 | tf_op jit(solution)/shard_map/last/pallas_call | solution.py:211
  105.9 0.0 copy-start
  105.9 1.3 copy-done
  107.2 4.2 %copy.8 = bf16[2048,512]{0,1:T(8,128)(2,1)} copy(bf16[2048,512]{1,0:T(8,128)(2,1)} %copy-done) | data formatting | bytes 4194304
  111.4 0.0 reduce-scatter.7.cloned.1.call-update
  111.4 34.3 %reduce-scatter.9.cloned.1.call-done = bf16[128,2048]{1,0:T(8,128)(2,1)} async-done(((bf16[512,2048]{1,0:T(8,128)(2,1)}), bf16[128,2048]{1,0:T(8,128)(2,1)}) %reduce-scatter.9.cloned.1.call-update) | async-done | bytes 524304
  145.7 1.3 copy.11
  147.1 43.7 %reduce-scatter.7.cloned.1.call-done = bf16[128,2048]{1,0:T(8,128)(2,1)} async-done(((bf16[512,2048]{1,0:T(8,128)(2,1)}), bf16[128,2048]{1,0:T(8,128)(2,1)}) %reduce-scatter.7.cloned.1.call-update) | async-done | bytes 524304
  190.7 1.3 copy.9
  192.1 1.0 pad_maximum_fusion
  (1 shorter events, 0.0 us)
Async XLA Ops:
  6.5 3.8 %copy-start.10 = (bf16[512,64]{0,1:T(8,128)(2,1)S(1)}, bf16[512,64]{0,1:T(8,128)(2,1)}, u32[]{:S(2)}) copy-start(bf16[512,64]{0,1:T(8,128)(2,1)} %param.6) | copy-start | bytes 196612
  6.5 42.0 %all-gather.5.cloned.1.call-start = ((), (), s32[]{:S(2)}) async-start(), calls=%async_computation.3 | async-start | bytes 4718592 | tf_op jit(solution)/shard_map/all_gather | solution.py:186
  8.9 78.2 %all-gather.3.cloned.1.call-start = ((), (), s32[]{:S(2)}) async-start(), calls=%async_computation.2 | async-start | bytes 4718592 | tf_op jit(solution)/shard_map/all_gather | solution.py:186
  9.6 136.1 %reduce-scatter.9.cloned.1.call-start = ((), (), s32[]{:S(2)}) async-start(), calls=%async_computation.5 | async-start | bytes 2621440
  48.6 0.6 copy-start.2
  49.2 0.7 copy-start.4
  49.9 0.7 copy-start.6
  50.5 0.6 copy-start.8
  51.2 35.9 %copy-start.3 = (s32[448]{0:T(512)S(1)}, s32[448]{0:T(512)}, u32[]{:S(2)}) copy-start(s32[448]{0:T(512)} %get-tuple-element.9.slot) | copy-start | bytes 5380
  51.2 35.9 %copy-start.5 = (s32[448]{0:T(512)S(1)}, s32[448]{0:T(512)}, u32[]{:S(2)}) copy-start(s32[448]{0:T(512)} %get-tuple-element.10.col) | copy-start | bytes 5380
  51.2 35.9 %copy-start.7 = (s32[112]{0:T(128)S(1)}, s32[112]{0:T(128)}, u32[]{:S(2)}) copy-start(s32[112]{0:T(128)} %get-tuple-element.11.row) | copy-start | bytes 1348
  51.2 35.9 %copy-start.9 = (s32[3]{0:T(128)S(1)}, s32[3]{0:T(128)}, u32[]{:S(2)}) copy-start(s32[3]{0:T(128)} %get-tuple-element.12.edge) | copy-start | bytes 40
  93.3 1.4 copy-start.1
  98.7 92.1 %reduce-scatter.7.cloned.1.call-start = ((), (), s32[]{:S(2)}) async-start(), calls=%async_computation.4 | async-start | bytes 2621440
  105.9 1.3 copy-start
Sparse Core Ops, SparseCore 0:
  9.2 39.2 all-gather.4
  50.4 36.5 all-gather.2
  98.8 46.8 reduce-scatter.8
  147.9 42.8 reduce-scatter.6

commit v2 on v1

v2 whole, which is shorter than its diff:
```python
import functools

import jax
import jax.numpy as jnp
from jax import lax
from jax.experimental import pallas as pl
from jax.experimental.pallas import tpu as pltpu
from jax.sharding import PartitionSpec as P

SPAN = 4
GROUP = 8


def row_cuts(brows):
    return (0, max(brows // 4, 1), brows)


def plan_kernel(coords, counts, slot_out, col_out, row_out, edge_out, seen, begin, *, brows, pad_col):
    count = counts[0]
    jobs = row_out.shape[0]

    def clear(r, _):
        seen[r] = 0
        return 0

    lax.fori_loop(0, brows, clear, 0)

    def tally(s, _):
        r = coords[0, s]
        seen[r] = seen[r] + 1
        return 0

    lax.fori_loop(0, count, tally, 0)

    cuts = row_cuts(brows)

    def blank(j, _):
        for k in range(SPAN):
            slot_out[j * SPAN + k] = 0
            col_out[j * SPAN + k] = pad_col
        row_out[j] = 0
        return 0

    lax.fori_loop(0, jobs, blank, 0)

    edge_out[0] = 0
    at = jnp.int32(0)
    for part in range(len(cuts) - 1):

        def lay(r, at):
            begin[r] = at * SPAN
            return at + (seen[r] + SPAN - 1) // SPAN

        first = at
        at = lax.fori_loop(cuts[part], cuts[part + 1], lay, at)
        at = first + (at - first + GROUP - 1) // GROUP * GROUP
        edge_out[part + 1] = at // GROUP

    def place(s, _):
        r = coords[0, s]
        spot = begin[r]
        begin[r] = spot + 1
        slot_out[spot] = s
        col_out[spot] = coords[1, s]
        row_out[spot // SPAN] = r
        return 0

    lax.fori_loop(0, count, place, 0)


def make_plan(coords, counts, brows, bcols):
    maxt = coords.shape[1]
    parts = len(row_cuts(brows)) - 1
    jobs = brows + -(-maxt // SPAN) + parts * GROUP
    jobs = -(-jobs // GROUP) * GROUP
    smem = pl.BlockSpec(memory_space=pltpu.SMEM)
    ints = lambda n: jax.ShapeDtypeStruct((n,), jnp.int32)
    return pl.pallas_call(
        functools.partial(plan_kernel, brows=brows, pad_col=bcols),
        out_shape=(ints(jobs * SPAN), ints(jobs * SPAN), ints(jobs), ints(parts + 1)),
        in_specs=[smem, smem],
        out_specs=(smem, smem, smem, smem),
        scratch_shapes=[pltpu.SMEM((brows,), jnp.int32), pltpu.SMEM((brows,), jnp.int32)],
        name="plan",
    )(coords, counts)


def apply_tiles(slot, col, row, edge, tiles, panel, acc, tbuf, pbuf, tsem, psem, lo, hi, first):
    tile = tiles.shape[1]
    per = GROUP * SPAN
    nodes = panel.shape[1]
    load = pltpu.make_async_copy(panel, pbuf.at[:, pl.ds(0, nodes)], psem)
    load.start()

    def fetch(g, _):
        for k in range(per):
            s = slot[g * per + k]
            pltpu.make_async_copy(
                tiles.at[s], tbuf.at[(g - lo) * per + k], tsem.at[g - lo]
            ).start()
        return 0

    lax.fori_loop(lo, hi, fetch, 0)
    pbuf[:, pl.ds(nodes, tile)] = jnp.zeros((pbuf.shape[0], tile), pbuf.dtype)
    acc[...] = jnp.zeros_like(acc)
    load.wait()

    def work(g, _):
        own = tbuf.at[pl.ds((g - lo) * per, per)]
        pltpu.make_async_copy(tiles.at[pl.ds(0, per)], own, tsem.at[g - lo]).wait()
        for j in range(GROUP):
            job = g * GROUP + j
            base = (g - lo) * per + j * SPAN
            lhs = jnp.concatenate([tbuf[base + k] for k in range(SPAN)], axis=1)
            rhs = jnp.concatenate(
                [
                    pbuf[:, pl.ds(pl.multiple_of(col[job * SPAN + k] * tile, tile), tile)]
                    for k in range(SPAN)
                ],
                axis=1,
            )
            prod = lax.dot_general(
                lhs, rhs, (((1,), (1,)), ((), ())), preferred_element_type=jnp.float32
            )
            spot = pl.ds(pl.multiple_of(jnp.maximum(row[job] - first, 0) * tile, tile), tile)
            acc[spot, :] = acc[spot, :] + prod
        return 0

    lax.fori_loop(lo, hi, work, 0)


def part_kernel(slot, col, row, edge, tiles, panel, weight, out, acc, tbuf, pbuf, tsem, psem, *, part, first):
    apply_tiles(
        slot, col, row, edge, tiles, panel, acc, tbuf, pbuf, tsem, psem,
        edge[part], edge[part + 1], first,
    )
    rows = acc.shape[0]
    ncol, _, fout = out.shape
    step = next(n for n in (512, 256, 128, rows) if rows % n == 0)
    for start in range(0, rows, step):
        spot = pl.ds(start, step)
        done = jnp.dot(
            acc[spot, :].astype(jnp.bfloat16), weight[...], preferred_element_type=jnp.float32
        ).astype(out.dtype)
        for c in range(ncol):
            out[c, spot, :] = done[:, c * fout : (c + 1) * fout]


def body(features, weight_t, tiles, coords, counts):
    maxt, tile, _ = tiles.shape
    nodes, wide = features.shape
    fout = weight_t.shape[0]
    nrow, ncol = lax.axis_size("row"), lax.axis_size("col")
    brows, bcols = nodes * ncol // nrow // tile, nodes // tile
    width = wide * nrow

    plan = make_plan(coords, counts, brows, bcols)
    jobs = plan[2].shape[0]
    panel = lax.all_gather(features, "row", axis=1, tiled=True).T
    weight = lax.all_gather(weight_t, "row", axis=1, tiled=True).T

    smem = pl.BlockSpec(memory_space=pltpu.SMEM)
    hbm = pl.BlockSpec(memory_space=pl.ANY)
    cuts = row_cuts(brows)
    outs = []
    for part, (low, high) in enumerate(zip(cuts[:-1], cuts[1:])):
        rows = (high - low) * tile
        shape = (ncol, rows, fout // ncol)
        partial = pl.pallas_call(
            functools.partial(part_kernel, part=part, first=low),
            grid=(1,),
            out_shape=jax.ShapeDtypeStruct(shape, jnp.bfloat16),
            in_specs=[smem] * 4 + [hbm, hbm, pl.BlockSpec(weight.shape, lambda i: (0, 0))],
            out_specs=pl.BlockSpec(shape, lambda i: (0, 0, 0)),
            scratch_shapes=[
                pltpu.VMEM((rows, width), jnp.float32),
                pltpu.VMEM((jobs * SPAN, tile, tile), jnp.bfloat16),
                pltpu.VMEM((width, nodes + tile), jnp.bfloat16),
                pltpu.SemaphoreType.DMA((jobs // GROUP,)),
                pltpu.SemaphoreType.DMA,
            ],
            compiler_params=pltpu.CompilerParams(vmem_limit_bytes=52 * 1024 * 1024),
            cost_estimate=pl.CostEstimate(
                flops=2 * maxt * tile * tile * width, transcendentals=0, bytes_accessed=1 << 24
            ),
            name="part",
        )(*plan, tiles, panel, weight)
        outs.append(lax.psum_scatter(partial, "col", scatter_dimension=0, tiled=False))
    return jnp.concatenate(outs, axis=0)


def solution(mesh):
    placed = (
        P("col", "row"),
        P(None, "row"),
        P(("row", "col"), None, None),
        P(None, ("row", "col")),
        P(("row", "col")),
    )
    return jax.shard_map(
        body, mesh=mesh, in_specs=placed, out_specs=P("row", "col"), check_vma=False
    )
```

time: 200 us -> 179 us (0.90)
  local copies, waits for them, and re-layouts: 18.4 us -> 2.58 us
  waiting for transfers between devices: 125 us -> 119 us
    unnamed x6 -> x3, waiting for transfers between devices: 78.7 us -> 0.74 us
    reduce_scatter x0 -> x2, waiting for transfers between devices: none -> 75.9 us  [body(): lax.psum_scatter(partial, 'col', scatter_dimension=0, tiled=False)]
    unnamed x26 -> x16, local copies, waits for them, and re-layouts: 16 us -> 2.58 us
    all_gather x2 -> x1, waiting for transfers between devices: 46.7 us -> 42.2 us  [body(): panel = lax.all_gather(features, 'row', axis=1, tiled=True).T]
    slice x1 -> x0, local copies, waits for them, and re-layouts: 2.31 us -> none  [body(): own = features[:, f * piece:(f + 1) * piece]]
    pallas_call x3 -> x2, Pallas kernels: 23.9 us -> 23.4 us  [body(): pl.pallas_call(functools.partial(part_kernel, part=part, first=low), grid...]
  transfers between devices with their start and end apart: 4 -> 3, of which waited for: 4 -> 3; matrix products, arithmetic and copies ran while one was open for 3% -> 0% of each run, Pallas kernels for 12% -> 12%
where the time goes in v2:
time: 179 us
  waiting for transfers between devices  119 us (66%)
  Pallas kernels  29.6 us (17%)
  between operations  13.8 us (8%)
  blocking collectives  12 us (7%)
  local copies, waits for them, and re-layouts  2.58 us (1%)
  other arithmetic  2.22 us (1%)
    reduce_scatter x2, waiting for transfers between devices, body(): lax.psum_scatter(partial, 'col', scatter_dimension=0, tiled=False)  75.9 us
    all_gather x1, waiting for transfers between devices, body(): panel = lax.all_gather(features, 'row', axis=1, tiled=True).T  42.2 us
    pallas_call x2, Pallas kernels, body(): pl.pallas_call(functools.partial(part_kernel, part=part, first=low), grid...  23.4 us
    all_gather x1, blocking collectives, body(): weight = lax.all_gather(weight_t, 'row', axis=1, tiled=True).T  12 us
    pallas_call x1, Pallas kernels, make_plan(): pl.pallas_call(functools.partial(plan_kernel, brows=brows, pad_col=bcols)...  6.16 us
  transfers between devices with their start and end apart: 3, of which 3 were waited for; matrix products, arithmetic and copies ran while one was open for 0% of the time, Pallas kernels for 12%

profile of v2, /device:TPU:0, one launch (start us, length us, event | category | flops | bytes accessed | tf_op | source)
XLA Modules:
  0.0 179.2 jit_solution(11749077073589367289)
XLA Ops:
  6.5 0.0 all-gather.2.cloned.1.call-start
  6.5 0.7 all-gather.2.cloned.1.call-update
  7.3 0.0 reduce-scatter.3.cloned.1.call-start
  7.9 6.2 %plan.1 = (s32[448]{0:T(512)}, s32[448]{0:T(512)}, s32[112]{0:T(128)}, s32[3]{0:T(128)}) custom-call(s32[2,256]{1,0:T(2,128)} %coords.1, s32[1]{0:T(128)S(6)} %copy.6.counts), custom_call_target="tpu_custom_call" | custom-call | tf_op jit(solution)/shard_map/plan/pallas_call | solution.py:78
  14.1 12.0 %all_gather.7 = bf16[512,512]{0,1:T(8,128)(2,1)S(1)} all-gather(bf16[512,64]{0,1:T(8,128)(2,1)} %param.6), channel_id=1, replica_groups=mesh['row'=8,'col'=4] {'row'}, dimensions={1}, use_global_device_ids=true | all-gather | bytes 589824 | tf_op jit(solution)/shard_map/all_gather | solution.py:160
  26.2 42.2 %all-gather.2.cloned.1.call-done = bf16[8192,512]{0,1:T(8,128)(2,1)} async-done(((bf16[8192,64]{0,1:T(8,128)(2,1)}), bf16[8192,512]{0,1:T(8,128)(2,1)}) %all-gather.2.cloned.1.call-update) | async-done | bytes 8388624 | tf_op jit(solution)/shard_map/all_gather | solution.py:159
  68.3 0.0 copy-start
  68.3 0.7 copy-done
  69.0 0.0 copy-start.2
  69.0 0.7 copy-done.2
  69.7 0.0 copy-start.4
  69.7 0.6 copy-done.4
  70.3 0.0 copy-start.6
  70.3 0.6 copy-done.6
  70.9 0.0 copy-start.1
  70.9 0.0 copy-start.3
  70.9 0.0 copy-start.5
  70.9 0.0 copy-start.7
  70.9 9.0 %part.2 = bf16[4,1024,128]{2,1,0:T(8,128)(2,1)} custom-call(s32[448]{0:T(512)S(1)} %copy-done, s32[448]{0:T(512)S(1)} %copy-done.2, s32[112]{0:T(128)S(1)} %copy-done.4, s32[3]{0:T(128)S(1)} %copy-done.6, bf16[256,128,128]{2,1,0:T(8,128)(2,1)} %tiles.3, bf16[512,8192]{1,0:T(8,128)(2,1)} %bitcast.6, bf16[512,512]{1,0:T(8,128)(2,1)S(1)} %bitcast.4), custom_call_target="tpu_custom_call" | custom-call | flops 4294967296 | bytes 16777216 | tf_op jit(solution)/shard_map/part/pallas_call | solution.py:169
  79.9 0.0 reduce-scatter.3.cloned.1.call-update
  79.9 0.0 reduce-scatter.5.cloned.1.call-start
  80.0 0.0 copy-done.1
  80.0 0.0 copy-done.3
  80.0 0.0 copy-done.5
  80.0 0.0 copy-done.7
  80.0 14.4 %part.3 = bf16[4,3072,128]{2,1,0:T(8,128)(2,1)} custom-call(s32[448]{0:T(512)S(1)} %copy-done.1, s32[448]{0:T(512)S(1)} %copy-done.3, s32[112]{0:T(128)S(1)} %copy-done.5, s32[3]{0:T(128)S(1)} %copy-done.7, bf16[256,128,128]{2,1,0:T(8,128)(2,1)} %tiles.3, bf16[512,8192]{1,0:T(8,128)(2,1)} %bitcast.7, bf16[512,512]{1,0:T(8,128)(2,1)S(1)} %bitcast.5), custom_call_target="tpu_custom_call" | custom-call | flops 4294967296 | bytes 16777216 | tf_op jit(solution)/shard_map/part/pallas_call | solution.py:169
  94.4 0.0 reduce-scatter.5.cloned.1.call-update
  94.5 14.7 %reduce-scatter.3.cloned.1.call-done = bf16[1,1024,128]{2,1,0:T(8,128)(2,1)} async-done(((bf16[4,1024,128]{2,1,0:T(8,128)(2,1)}), bf16[1,1024,128]{2,1,0:T(8,128)(2,1)}) %reduce-scatter.3.cloned.1.call-update) | async-done | bytes 262160 | tf_op jit(solution)/shard_map/reduce_scatter | solution.py:188
  109.2 61.2 %reduce-scatter.5.cloned.1.call-done = bf16[1,3072,128]{2,1,0:T(8,128)(2,1)} async-done(((bf16[4,3072,128]{2,1,0:T(8,128)(2,1)}), bf16[1,3072,128]{2,1,0:T(8,128)(2,1)}) %reduce-scatter.5.cloned.1.call-update) | async-done | bytes 786448 | tf_op jit(solution)/shard_map/reduce_scatter | solution.py:188
  170.4 2.2 %pad_maximum_fusion = bf16[4096,128]{1,0:T(8,128)(2,1)} fusion(bf16[3072,128]{1,0:T(8,128)(2,1)} %bitcast.8, bf16[1024,128]{1,0:T(8,128)(2,1)} %bitcast.9), kind=kLoop, calls=%fused_computation | loop fusion | flops 2097152 | bytes 2097152 | tf_op jit(solution)/shard_map/concatenate | solution.py:189
Async XLA Ops:
  6.5 61.8 %all-gather.2.cloned.1.call-start = ((), (), s32[]{:S(2)}) async-start(), calls=%async_computation.2 | async-start | bytes 9437184 | tf_op jit(solution)/shard_map/all_gather | solution.py:159
  7.3 101.9 %reduce-scatter.3.cloned.1.call-start = ((), (), s32[]{:S(2)}) async-start(), calls=%async_computation.3 | async-start | bytes 1310720 | tf_op jit(solution)/shard_map/reduce_scatter | solution.py:188
  68.3 0.7 copy-start
  69.0 0.7 copy-start.2
  69.7 0.6 copy-start.4
  70.3 0.6 copy-start.6
  70.9 9.0 %copy-start.1 = (s32[448]{0:T(512)S(1)}, s32[448]{0:T(512)}, u32[]{:S(2)}) copy-start(s32[448]{0:T(512)} %get-tuple-element.9.slot) | copy-start | bytes 5380
  70.9 9.1 %copy-start.3 = (s32[448]{0:T(512)S(1)}, s32[448]{0:T(512)}, u32[]{:S(2)}) copy-start(s32[448]{0:T(512)} %get-tuple-element.10.col) | copy-start | bytes 5380
  70.9 9.1 %copy-start.5 = (s32[112]{0:T(128)S(1)}, s32[112]{0:T(128)}, u32[]{:S(2)}) copy-start(s32[112]{0:T(128)} %get-tuple-element.11.row) | copy-start | bytes 1348
  70.9 9.1 %copy-start.7 = (s32[3]{0:T(128)S(1)}, s32[3]{0:T(128)}, u32[]{:S(2)}) copy-start(s32[3]{0:T(128)} %get-tuple-element.12.edge) | copy-start | bytes 40
  79.9 90.5 %reduce-scatter.5.cloned.1.call-start = ((), (), s32[]{:S(2)}) async-start(), calls=%async_computation.4 | async-start | bytes 3932160 | tf_op jit(solution)/shard_map/reduce_scatter | solution.py:188
Sparse Core Ops, SparseCore 0:
  9.2 59.0 all-gather.1
  80.0 29.1 reduce-scatter.2
  111.5 58.8 reduce-scatter.4

commit v3 on v2

v3 whole, which is shorter than its diff:
```python
import functools

import jax
import jax.numpy as jnp
from jax import lax
from jax.experimental import pallas as pl
from jax.experimental.pallas import tpu as pltpu
from jax.sharding import PartitionSpec as P

SPAN = 4
GROUP = 8


def row_cuts(brows):
    return (0, max(brows // 4, 1), brows)


def table_spots(jobs):
    return 0, jobs * SPAN, 2 * jobs * SPAN, (2 * SPAN + 1) * jobs


def plan_kernel(coords, counts, table, seen, begin, *, brows, pad_col, jobs):
    count = counts[0]
    slot_at, col_at, row_at, edge_at = table_spots(jobs)

    def clear(r, _):
        seen[r] = 0
        return 0

    lax.fori_loop(0, brows, clear, 0)

    def tally(s, _):
        r = coords[0, s]
        seen[r] = seen[r] + 1
        return 0

    lax.fori_loop(0, count, tally, 0)

    cuts = row_cuts(brows)

    def blank(j, _):
        for k in range(SPAN):
            table[slot_at + j * SPAN + k] = 0
            table[col_at + j * SPAN + k] = pad_col
        table[row_at + j] = 0
        return 0

    lax.fori_loop(0, jobs, blank, 0)

    table[edge_at] = 0
    at = jnp.int32(0)
    for part in range(len(cuts) - 1):

        def lay(r, at):
            begin[r] = at * SPAN
            return at + (seen[r] + SPAN - 1) // SPAN

        first = at
        at = lax.fori_loop(cuts[part], cuts[part + 1], lay, at)
        at = first + (at - first + GROUP - 1) // GROUP * GROUP
        table[edge_at + part + 1] = at // GROUP

    def place(s, _):
        r = coords[0, s]
        spot = begin[r]
        begin[r] = spot + 1
        table[slot_at + spot] = s
        table[col_at + spot] = coords[1, s]
        table[row_at + spot // SPAN] = r
        return 0

    lax.fori_loop(0, count, place, 0)


def make_plan(coords, counts, brows, bcols):
    maxt = coords.shape[1]
    parts = len(row_cuts(brows)) - 1
    jobs = brows + -(-maxt // SPAN) + parts * GROUP
    jobs = -(-jobs // GROUP) * GROUP
    smem = pl.BlockSpec(memory_space=pltpu.SMEM)
    size = table_spots(jobs)[-1] + parts + 1
    table = pl.pallas_call(
        functools.partial(plan_kernel, brows=brows, pad_col=bcols, jobs=jobs),
        out_shape=jax.ShapeDtypeStruct((size,), jnp.int32),
        in_specs=[smem, smem],
        out_specs=smem,
        scratch_shapes=[pltpu.SMEM((brows,), jnp.int32), pltpu.SMEM((brows,), jnp.int32)],
        name="plan",
    )(coords, counts)
    return table, jobs


def apply_tiles(table, jobs, tiles, panel, acc, tbuf, pbuf, tsem, psem, part, first):
    slot_at, col_at, row_at, edge_at = table_spots(jobs)
    lo, hi = table[edge_at + part], table[edge_at + part + 1]
    tile = tiles.shape[1]
    per = GROUP * SPAN
    nodes = panel.shape[1]
    half = panel.shape[0] // 2
    loads = [
        pltpu.make_async_copy(
            panel.at[pl.ds(h * half, half)],
            pbuf.at[pl.ds(h * half, half), pl.ds(0, nodes)],
            psem.at[h],
        )
        for h in range(2)
    ]
    loads[0].start()

    def fetch(g, _):
        for k in range(per):
            s = table[slot_at + g * per + k]
            pltpu.make_async_copy(
                tiles.at[s], tbuf.at[(g - lo) * per + k], tsem.at[g - lo]
            ).start()
        return 0

    lax.fori_loop(lo, hi, fetch, 0)
    loads[1].start()
    pbuf[:, pl.ds(nodes, tile)] = jnp.zeros((pbuf.shape[0], tile), pbuf.dtype)
    acc[...] = jnp.zeros_like(acc)

    def work(g, _, h):
        own = tbuf.at[pl.ds((g - lo) * per, per)]
        if h == 0:
            pltpu.make_async_copy(tiles.at[pl.ds(0, per)], own, tsem.at[g - lo]).wait()
        side = pl.ds(h * half, half)
        for j in range(GROUP):
            job = g * GROUP + j
            base = (g - lo) * per + j * SPAN
            lhs = jnp.concatenate([tbuf[base + k] for k in range(SPAN)], axis=1)
            cols = [
                pl.ds(pl.multiple_of(table[col_at + job * SPAN + k] * tile, tile), tile)
                for k in range(SPAN)
            ]
            rhs = jnp.concatenate([pbuf[side, col] for col in cols], axis=1)
            prod = lax.dot_general(
                lhs, rhs, (((1,), (1,)), ((), ())), preferred_element_type=jnp.float32
            )
            at = jnp.maximum(table[row_at + job] - first, 0) * tile
            spot = pl.ds(pl.multiple_of(at, tile), tile)
            acc[spot, side] = acc[spot, side] + prod
        return 0

    for h in range(2):
        loads[h].wait()
        lax.fori_loop(lo, hi, functools.partial(work, h=h), 0)


def part_kernel(table, tiles, panel, weight, out, acc, tbuf, pbuf, tsem, psem, *, jobs, part, first):
    apply_tiles(
        table, jobs, tiles, panel, acc, tbuf, pbuf, tsem, psem, part, first
    )
    rows = acc.shape[0]
    ncol, _, fout = out.shape
    step = next(n for n in (512, 256, 128, rows) if rows % n == 0)
    for start in range(0, rows, step):
        spot = pl.ds(start, step)
        done = jnp.dot(
            acc[spot, :].astype(jnp.bfloat16), weight[...], preferred_element_type=jnp.float32
        ).astype(out.dtype)
        for c in range(ncol):
            out[c, spot, :] = done[:, c * fout : (c + 1) * fout]


def body(features, weight_t, tiles, coords, counts):
    maxt, tile, _ = tiles.shape
    nodes, wide = features.shape
    fout = weight_t.shape[0]
    nrow, ncol = lax.axis_size("row"), lax.axis_size("col")
    brows, bcols = nodes * ncol // nrow // tile, nodes // tile
    width = wide * nrow

    table, jobs = make_plan(coords, counts, brows, bcols)
    panel = lax.all_gather(features, "row", axis=1, tiled=True).T
    weight = lax.all_gather(weight_t, "row", axis=1, tiled=True).T

    smem = pl.BlockSpec(memory_space=pltpu.SMEM)
    hbm = pl.BlockSpec(memory_space=pl.ANY)
    cuts = row_cuts(brows)
    outs = []
    for part, (low, high) in enumerate(zip(cuts[:-1], cuts[1:])):
        rows = (high - low) * tile
        shape = (ncol, rows, fout // ncol)
        partial = pl.pallas_call(
            functools.partial(part_kernel, jobs=jobs, part=part, first=low),
            grid=(1,),
            out_shape=jax.ShapeDtypeStruct(shape, jnp.bfloat16),
            in_specs=[smem, hbm, hbm, pl.BlockSpec(weight.shape, lambda i: (0, 0))],
            out_specs=pl.BlockSpec(shape, lambda i: (0, 0, 0)),
            scratch_shapes=[
                pltpu.VMEM((rows, width), jnp.float32),
                pltpu.VMEM((jobs * SPAN, tile, tile), jnp.bfloat16),
                pltpu.VMEM((width, nodes + tile), jnp.bfloat16),
                pltpu.SemaphoreType.DMA((jobs // GROUP,)),
                pltpu.SemaphoreType.DMA((2,)),
            ],
            compiler_params=pltpu.CompilerParams(vmem_limit_bytes=52 * 1024 * 1024),
            cost_estimate=pl.CostEstimate(
                flops=2 * maxt * tile * tile * width, transcendentals=0, bytes_accessed=1 << 24
            ),
            name="part",
        )(table, tiles, panel, weight)
        outs.append(lax.psum_scatter(partial, "col", scatter_dimension=0, tiled=False))
    return jnp.concatenate(outs, axis=0)


def solution(mesh):
    placed = (
        P("col", "row"),
        P(None, "row"),
        P(("row", "col"), None, None),
        P(None, ("row", "col")),
        P(("row", "col")),
    )
    return jax.shard_map(
        body, mesh=mesh, in_specs=placed, out_specs=P("row", "col"), check_vma=False
    )
```

time: 179 us -> 177 us (0.989)
  blocking collectives: 12 us -> 20 us
  Pallas kernels: 29.6 us -> 25.1 us
  waiting for transfers between devices: 119 us -> 116 us
  local copies, waits for them, and re-layouts: 2.58 us -> 0.69 us
    all_gather x1, blocking collectives: 12 us -> 20 us  [body(): weight = lax.all_gather(weight_t, 'row', axis=1, tiled=True).T]
    all_gather x1, waiting for transfers between devices: 42.2 us -> 36.3 us  [body(): panel = lax.all_gather(features, 'row', axis=1, tiled=True).T]
    pallas_call x3, Pallas kernels: 29.6 us -> 25.1 us  [the longest x2 21 us: body(): pl.pallas_call(functools.partial(part_kernel, jobs=jobs, part=part, first...]
    reduce_scatter x2, waiting for transfers between devices: 75.9 us -> 78.7 us  [body(): lax.psum_scatter(partial, 'col', scatter_dimension=0, tiled=False)]
    unnamed x16 -> x4, local copies, waits for them, and re-layouts: 2.58 us -> 0.69 us
  transfers between devices with their start and end apart: 3 -> 3, of which waited for: 3 -> 3; matrix products, arithmetic and copies ran while one was open for 0% -> 0% of each run, Pallas kernels for 12% -> 10%
where the time goes in v3:
time: 177 us; the launch traced here: 178 us
  waiting for transfers between devices  116 us (66%)
  Pallas kernels  25.1 us (14%)
  blocking collectives  20 us (11%)
  between operations  13.8 us (8%)
  other arithmetic  2.22 us (1%)
    reduce_scatter x2, waiting for transfers between devices, body(): lax.psum_scatter(partial, 'col', scatter_dimension=0, tiled=False)  78.7 us
    all_gather x1, waiting for transfers between devices, body(): panel = lax.all_gather(features, 'row', axis=1, tiled=True).T  36.3 us
    pallas_call x2, Pallas kernels, body(): pl.pallas_call(functools.partial(part_kernel, jobs=jobs, part=part, first...  21 us
    all_gather x1, blocking collectives, body(): weight = lax.all_gather(weight_t, 'row', axis=1, tiled=True).T  20 us
    pallas_call x1, Pallas kernels, make_plan(): pl.pallas_call(functools.partial(plan_kernel, brows=brows, pad_col=bcols,...  4.08 us
  transfers between devices with their start and end apart: 3, of which 3 were waited for; matrix products, arithmetic and copies ran while one was open for 0% of the time, Pallas kernels for 10%

profile of v3, /device:TPU:0, one launch (start us, length us, event | category | flops | bytes accessed | tf_op | source)
XLA Modules:
  0.0 177.6 jit_solution(5220308157964352686)
XLA Ops:
  6.5 0.0 all-gather.2.cloned.1.call-start
  6.5 0.7 all-gather.2.cloned.1.call-update
  7.3 0.0 reduce-scatter.3.cloned.1.call-start
  7.9 4.1 %plan.1.table = s32[1011]{0:T(1024)} custom-call(s32[2,256]{1,0:T(2,128)} %coords.1, s32[1]{0:T(128)S(6)} %copy.6.counts), custom_call_target="tpu_custom_call" | custom-call | tf_op jit(solution)/shard_map/plan/pallas_call | solution.py:82
  12.0 20.0 %all_gather.7 = bf16[512,512]{0,1:T(8,128)(2,1)S(1)} all-gather(bf16[512,64]{0,1:T(8,128)(2,1)} %param.6), channel_id=1, replica_groups=mesh['row'=8,'col'=4] {'row'}, dimensions={1}, use_global_device_ids=true | all-gather | bytes 589824 | tf_op jit(solution)/shard_map/all_gather | solution.py:176
  32.1 36.3 %all-gather.2.cloned.1.call-done = bf16[8192,512]{0,1:T(8,128)(2,1)} async-done(((bf16[8192,64]{0,1:T(8,128)(2,1)}), bf16[8192,512]{0,1:T(8,128)(2,1)}) %all-gather.2.cloned.1.call-update) | async-done | bytes 8388624 | tf_op jit(solution)/shard_map/all_gather | solution.py:175
  68.3 0.0 copy-start
  68.3 0.7 copy-done
  69.0 0.0 copy-start.1
  69.0 7.9 %part.2 = bf16[4,1024,128]{2,1,0:T(8,128)(2,1)} custom-call(s32[1011]{0:T(1024)S(1)} %copy-done, bf16[256,128,128]{2,1,0:T(8,128)(2,1)} %tiles.3, bf16[512,8192]{1,0:T(8,128)(2,1)} %bitcast.6, bf16[512,512]{1,0:T(8,128)(2,1)S(1)} %bitcast.4), custom_call_target="tpu_custom_call" | custom-call | flops 4294967296 | bytes 16777216 | tf_op jit(solution)/shard_map/part/pallas_call | solution.py:185
  76.9 0.0 reduce-scatter.3.cloned.1.call-update
  77.0 0.0 reduce-scatter.5.cloned.1.call-start
  77.0 0.0 copy-done.1
  77.0 13.1 %part.3 = bf16[4,3072,128]{2,1,0:T(8,128)(2,1)} custom-call(s32[1011]{0:T(1024)S(1)} %copy-done.1, bf16[256,128,128]{2,1,0:T(8,128)(2,1)} %tiles.3, bf16[512,8192]{1,0:T(8,128)(2,1)} %bitcast.7, bf16[512,512]{1,0:T(8,128)(2,1)S(1)} %bitcast.5), custom_call_target="tpu_custom_call" | custom-call | flops 4294967296 | bytes 16777216 | tf_op jit(solution)/shard_map/part/pallas_call | solution.py:185
  90.1 0.0 reduce-scatter.5.cloned.1.call-update
  90.2 17.4 %reduce-scatter.3.cloned.1.call-done = bf16[1,1024,128]{2,1,0:T(8,128)(2,1)} async-done(((bf16[4,1024,128]{2,1,0:T(8,128)(2,1)}), bf16[1,1024,128]{2,1,0:T(8,128)(2,1)}) %reduce-scatter.3.cloned.1.call-update) | async-done | bytes 262160 | tf_op jit(solution)/shard_map/reduce_scatter | solution.py:204
  107.6 61.3 %reduce-scatter.5.cloned.1.call-done = bf16[1,3072,128]{2,1,0:T(8,128)(2,1)} async-done(((bf16[4,3072,128]{2,1,0:T(8,128)(2,1)}), bf16[1,3072,128]{2,1,0:T(8,128)(2,1)}) %reduce-scatter.5.cloned.1.call-update) | async-done | bytes 786448 | tf_op jit(solution)/shard_map/reduce_scatter | solution.py:204
  168.9 2.2 %pad_maximum_fusion = bf16[4096,128]{1,0:T(8,128)(2,1)} fusion(bf16[3072,128]{1,0:T(8,128)(2,1)} %bitcast.8, bf16[1024,128]{1,0:T(8,128)(2,1)} %bitcast.9), kind=kLoop, calls=%fused_computation | loop fusion | flops 2097152 | bytes 2097152 | tf_op jit(solution)/shard_map/concatenate | solution.py:205
Async XLA Ops:
  6.5 61.8 %all-gather.2.cloned.1.call-start = ((), (), s32[]{:S(2)}) async-start(), calls=%async_computation.2 | async-start | bytes 9437184 | tf_op jit(solution)/shard_map/all_gather | solution.py:175
  7.3 100.3 %reduce-scatter.3.cloned.1.call-start = ((), (), s32[]{:S(2)}) async-start(), calls=%async_computation.3 | async-start | bytes 1310720 | tf_op jit(solution)/shard_map/reduce_scatter | solution.py:204
  68.3 0.7 copy-start
  69.0 8.0 %copy-start.1 = (s32[1011]{0:T(1024)S(1)}, s32[1011]{0:T(1024)}, u32[]{:S(2)}) copy-start(s32[1011]{0:T(1024)} %plan.1.table) | copy-start | bytes 12136
  77.0 91.9 %reduce-scatter.5.cloned.1.call-start = ((), (), s32[]{:S(2)}) async-start(), calls=%async_computation.4 | async-start | bytes 3932160 | tf_op jit(solution)/shard_map/reduce_scatter | solution.py:204
Sparse Core Ops, SparseCore 0:
  9.2 59.0 all-gather.1
  77.1 30.4 reduce-scatter.2
  109.9 58.9 reduce-scatter.4
